TPU v7x, 256 devices: a whole 4x4x8 slice. The times are simulated.
256 devices in a mesh: frame: 32 (over y, z_hi, core), pos: 8 (over z_lo, x).
Axes of the slice: x: 4, y: 4, z: 8 (z_hi: 4, z_lo: 2; z = z_hi * 2 + z_lo), core: 2. Of those that a mesh axis runs over, the one named last changes fastest.
Arguments:
- spatial_qkv: bfloat16 [2, 32, 1536, 3, 1152], P(None, 'frame', 'pos'), may hold values from -9 to 9
- residual: bfloat16 [2, 32, 1536, 1152], P(None, 'frame', 'pos'), may hold values from -0.59765625 to 0.59765625
- spatial_gate: float32 [2, 1152], replicated, may hold values from 0.5 to 2
- spatial_proj: bfloat16 [1152, 1152], replicated, may hold values from -0.1875 to 0.1875
- spatial_qgain: float32 [72], replicated, may hold values from 0.5 to 8
- spatial_kgain: float32 [72], replicated, may hold values from 0.5 to 8
- temporal_shift: float32 [2, 1152], replicated, may hold values from -3 to 3
- temporal_scale: float32 [2, 1152], replicated, may hold values from -0.5 to 0.5
- temporal_qkv: bfloat16 [1152, 3456], replicated, as said below
- temporal_qgain: float32 [72], replicated, may hold values from 0.6 to 6
- temporal_kgain: float32 [72], replicated, may hold values from 0.6 to 6
Outputs:
- temporal_out: bfloat16 [2, 32, 1536, 1152], P(None, 'frame', 'pos')
Inputs may be any that keep to these rules, and one draw needn't show every extreme that they name: `temporal_qkv`: entries are of the size of a weight with fan-in 1152.
All inputs are finite; a program needn't handle non-finite values.
Results may differ from a plain program's by a relative error of at most 0.028.
The roundings to bfloat16 on the way count: a program that leaves them out, or rounds other values in their place, can miss the bound.
Values may be sent and summed in bfloat16 or wider, within the bound.
A program may use at most 128 MiB of HBM per device.

v0:
```python
import math

import jax
import jax.numpy as jnp
from jax import lax
from jax.sharding import PartitionSpec as P

EPSILON = 1e-06


def head_norm(values, gain):
    widened = values.astype(jnp.float32)
    factor = lax.rsqrt(jnp.mean(widened * widened, axis=-1, keepdims=True) + EPSILON)
    return (widened * factor * gain).astype(jnp.bfloat16)


def softmax_weights(scores):
    row_top = jnp.max(scores, axis=-1, keepdims=True)
    expons = jnp.exp(scores - row_top)
    return (expons / jnp.sum(expons, axis=-1, keepdims=True)).astype(jnp.bfloat16)


def spatial_attend(element, query_gain, keys_gain):
    query_norm = head_norm(element[:, 0], query_gain)
    keys_norm = head_norm(element[:, 1], keys_gain)
    scores = jnp.einsum(
        "qhd,khd->hqk", query_norm, keys_norm, preferred_element_type=jnp.float32
    ) / math.sqrt(element.shape[-1])
    weights = softmax_weights(scores)
    return jnp.einsum(
        "hqk,khd->qhd", weights, element[:, 2], preferred_element_type=jnp.float32
    ).astype(jnp.bfloat16)


def per_device(
    spatial_qkv,
    residual,
    spatial_gate,
    spatial_proj,
    spatial_qgain,
    spatial_kgain,
    temporal_shift,
    temporal_scale,
    temporal_qkv,
    temporal_qgain,
    temporal_kgain,
):
    videos, frames_loc, pos_loc, triple, width = spatial_qkv.shape
    head_dim = spatial_qgain.shape[0]
    heads = width // head_dim
    pos_count = lax.axis_size("pos")
    frame_count = lax.axis_size("frame")
    heads_loc = heads // pos_count
    group_width = heads_loc * head_dim
    entries = videos * frames_loc
    all_pos = pos_count * pos_loc
    packed = spatial_qkv.reshape(entries, 1, pos_loc, 3, pos_count, group_width)
    by_heads = lax.all_to_all(packed, "pos", split_axis=4, concat_axis=1, tiled=True)
    by_heads = by_heads.reshape(entries, all_pos, 3, heads_loc, head_dim)
    attended = lax.map(
        lambda element: spatial_attend(element, spatial_qgain, spatial_kgain), by_heads
    )
    outgoing = attended.reshape(entries, pos_count, pos_loc, 1, group_width)
    returned = lax.all_to_all(outgoing, "pos", split_axis=1, concat_axis=3, tiled=True)
    mixed = jnp.dot(
        returned.reshape(entries * pos_loc, width), spatial_proj, preferred_element_type=jnp.float32
    )
    mixed = mixed.reshape(videos, frames_loc, pos_loc, width)
    updated = (residual.astype(jnp.float32) + spatial_gate[:, None, None, :] * mixed).astype(
        jnp.bfloat16
    )
    widened = updated.astype(jnp.float32)
    centred = widened - jnp.mean(widened, axis=-1, keepdims=True)
    spread = jnp.mean(centred * centred, axis=-1, keepdims=True)
    scaled = centred * lax.rsqrt(spread + EPSILON) * (1.0 + temporal_scale[:, None, None, :])
    normed = (scaled + temporal_shift[:, None, None, :]).astype(jnp.bfloat16)
    pos_group = pos_loc // frame_count
    frames_all = frames_loc * frame_count
    moved = lax.all_to_all(normed, "frame", split_axis=2, concat_axis=1, tiled=True)
    by_frames = jnp.dot(
        moved.reshape(videos * frames_all * pos_group, width),
        temporal_qkv,
        preferred_element_type=jnp.float32,
    )
    by_frames = by_frames.astype(jnp.bfloat16)
    arranged = by_frames.reshape(videos, frames_all, pos_group, 3, heads, head_dim)
    query_norm = head_norm(arranged[:, :, :, 0], temporal_qgain)
    keys_norm = head_norm(arranged[:, :, :, 1], temporal_kgain)
    scores = jnp.einsum(
        "bfphd,bgphd->bphfg", query_norm, keys_norm, preferred_element_type=jnp.float32
    ) / math.sqrt(head_dim)
    weights = softmax_weights(scores)
    result = jnp.einsum(
        "bphfg,bgphd->bfphd", weights, arranged[:, :, :, 2], preferred_element_type=jnp.float32
    )
    result = result.astype(jnp.bfloat16).reshape(videos, frames_all, pos_group, width)
    return lax.all_to_all(result, "frame", split_axis=1, concat_axis=2, tiled=True)


def solution(mesh):
    return jax.shard_map(
        per_device,
        mesh=mesh,
        in_specs=(
            P(None, "frame", "pos", None, None),
            P(None, "frame", "pos", None),
            P(),
            P(),
            P(),
            P(),
            P(),
            P(),
            P(),
            P(),
            P(),
        ),
        out_specs=P(None, "frame", "pos", None),
        check_vma=False,
    )
```

profile of v0, /device:TPU:1, one launch (start us, length us, event | category | flops | bytes accessed | tf_op | source)
XLA Modules:
  0.0 258.9 jit_solution(10266943227910569294)
XLA Ops:
  0.0 5.6 %copy.81 = bf16[2,1,192,3,1152]{2,4,3,0,1:T(8,128)(2,1)} copy(bf16[2,1,192,3,1152]{4,2,3,1,0:T(8,128)(2,1)} %param.13) | data formatting | bytes 5308416 | tf_op args[0]
  5.6 4.1 %copy.82 = bf16[2,1,192,3,8,144]{2,5,3,0,1,4:T(8,128)(2,1)} copy(bf16[2,1,192,3,8,144]{2,5,4,3,0,1:T(8,128)(2,1)} %bitcast.114) | data formatting | bytes 5308416 | tf_op jit(solution)/shard_map/reshape | solution.py:57
  9.7 6.2 %all-to-all-start = ((bf16[2,1,192,3,8,144]{2,5,3,0,1,4:T(8,128)(2,1)}), bf16[2,1,192,3,8,144]{2,5,3,0,1,4:T(8,128)(2,1)}, u32[]{:S(2)}, u32[]{:S(2)}) async-start(bf16[2,1,192,3,8,144]{2,5,3,0,1,4:T(8,128)(2,1)} %copy.82), calls=%async_computation | async-start | bytes 7077888 | tf_op jit(solution)/shard_map/all_to_all | solution.py:58
  15.9 41.8 %all-to-all-done = bf16[2,1,192,3,8,144]{2,5,3,0,1,4:T(8,128)(2,1)} async-done(((bf16[2,1,192,3,8,144]{2,5,3,0,1,4:T(8,128)(2,1)}), bf16[2,1,192,3,8,144]{2,5,3,0,1,4:T(8,128)(2,1)}, u32[]{:S(2)}, u32[]{:S(2)}) %all-to-all-start) | async-done | bytes 2654240 | tf_op jit(solution)/shard_map/all_to_all | solution.py:58
  57.7 5.8 %copy.83 = bf16[2,8,1,192,3,1,144]{3,1,6,4,0,5,2:T(8,128)(2,1)} copy(bf16[2,8,1,192,3,1,144]{3,6,4,0,1,5,2:T(8,128)(2,1)} %bitcast.11) | data formatting | bytes 5308416 | tf_op jit(solution)/shard_map/all_to_all | solution.py:58
  63.5 6.4 %reshape.114 = bf16[2,1536,3,2,72]{1,4,3,2,0:T(8,128)(2,1)} reshape(bf16[2,8,1,192,3,1,144]{3,1,6,4,0,5,2:T(8,128)(2,1)} %copy.83) | data formatting | bytes 5308416 | tf_op jit(solution)/shard_map/reshape | solution.py:59
  69.8 55.8 %while.10 = (s32[]{:T(128)}, bf16[2,1536,2,72]{1,3,2,0:T(8,128)(2,1)}, bf16[2,1536,3,2,72]{1,4,3,2,0:T(8,128)(2,1)}, f32[72]{0:T(128)S(1)}, f32[72]{0:T(128)S(1)}, /*index=5*/s32[]{:T(128)}) while((s32[]{:T(128)}, bf16[2,1536,2,72]{1,3,2,0:T(8,128)(2,1)}, bf16[2,1536,3,2,72]{1,4,3,2,0:T(8,128)(2,1)}, f32[72]{0:T(128)S(1)}, f32[72]{0:T(128)S(1)}, ...), condition=%wide.region_5.6_spmd, body=%wide.region_0.5_spmd.sunk | while | flops 2076561408 | bytes 49399972 | solution.py:60
  69.8 1.4 dynamic-slice_bitcast_fusion.2
  72.4 8.0 %fusion.83 = f32[2,1536,1536]{1,2,0:T(8,128)} fusion(f32[72]{0:T(128)S(1)} %get-tuple-element.111, f32[1536,2]{0,1:T(2,128)S(1)} %get-tuple-element.93, bf16[1536,3,2,72]{0,3,2,1:T(8,128)(2,1)S(1)} %dynamic-slice_bitcast_fusion.2, f32[72]{0:T(128)S(1)} %get-tuple-element.110, f32[1536,2]{0,1:T(2,128)S(1)} %get-tuple-element.94), kind=kOutput, calls=%fused_computation.25.clone.1 | convolution fusion | flops 681246720 | bytes 19784704 | tf_op jit(solution)/shard_map/while/body/eval_jaxpr/qhd,khd->hqk/dot_general | solution.py:26
  80.4 7.0 %fusion.82 = f32[2,1536]{1,0:T(2,128)S(1)} fusion(f32[72]{0:T(128)S(1)} %get-tuple-element.111, f32[1536,2]{0,1:T(2,128)S(1)} %get-tuple-element.93, bf16[1536,3,2,72]{0,3,2,1:T(8,128)(2,1)} %copy-done.1, f32[72]{0:T(128)S(1)} %get-tuple-element.110, f32[1536,2]{0,1:T(2,128)S(1)} %get-tuple-element.94), kind=kOutput, calls=%fused_computation.73.clone.1 | convolution fusion | flops 695404032 | bytes 922176 | tf_op jit(solution)/shard_map/while/body/eval_jaxpr/sub | solution.py:19
  87.3 10.4 %fusion.84 = bf16[2,1536,2,72]{1,3,2,0:T(8,128)(2,1)} fusion(bf16[2,1536,2,72]{1,3,2,0:T(8,128)(2,1)} %get-tuple-element.102, s32[]{:T(128)} %get-tuple-element.101, f32[2,1536]{1,0:T(2,128)S(1)} %fusion.82, f32[2,1536,1536]{1,2,0:T(8,128)} %fusion.83, bf16[1536,3,2,72]{0,3,2,1:T(8,128)(2,1)} %copy-done.1), kind=kOutput, calls=%fused_computation.9.clone.1 | convolution fusion | flops 698577408 | bytes 19771904 | tf_op jit(solution)/shard_map/while/body/eval_jaxpr/hqk,khd->qhd/dot_general | solution.py:30
  97.7 1.4 dynamic-slice_bitcast_fusion.2
  100.3 8.0 %fusion.83 = f32[2,1536,1536]{1,2,0:T(8,128)} fusion(f32[72]{0:T(128)S(1)} %get-tuple-element.111, f32[1536,2]{0,1:T(2,128)S(1)} %get-tuple-element.93, bf16[1536,3,2,72]{0,3,2,1:T(8,128)(2,1)S(1)} %dynamic-slice_bitcast_fusion.2, f32[72]{0:T(128)S(1)} %get-tuple-element.110, f32[1536,2]{0,1:T(2,128)S(1)} %get-tuple-element.94), kind=kOutput, calls=%fused_computation.25.clone.1 | convolution fusion | flops 681246720 | bytes 19784704 | tf_op jit(solution)/shard_map/while/body/eval_jaxpr/qhd,khd->hqk/dot_general | solution.py:26
  108.2 7.0 %fusion.82 = f32[2,1536]{1,0:T(2,128)S(1)} fusion(f32[72]{0:T(128)S(1)} %get-tuple-element.111, f32[1536,2]{0,1:T(2,128)S(1)} %get-tuple-element.93, bf16[1536,3,2,72]{0,3,2,1:T(8,128)(2,1)} %copy-done.1, f32[72]{0:T(128)S(1)} %get-tuple-element.110, f32[1536,2]{0,1:T(2,128)S(1)} %get-tuple-element.94), kind=kOutput, calls=%fused_computation.73.clone.1 | convolution fusion | flops 695404032 | bytes 922176 | tf_op jit(solution)/shard_map/while/body/eval_jaxpr/sub | solution.py:19
  115.2 10.4 %fusion.84 = bf16[2,1536,2,72]{1,3,2,0:T(8,128)(2,1)} fusion(bf16[2,1536,2,72]{1,3,2,0:T(8,128)(2,1)} %get-tuple-element.102, s32[]{:T(128)} %get-tuple-element.101, f32[2,1536]{1,0:T(2,128)S(1)} %fusion.82, f32[2,1536,1536]{1,2,0:T(8,128)} %fusion.83, bf16[1536,3,2,72]{0,3,2,1:T(8,128)(2,1)} %copy-done.1), kind=kOutput, calls=%fused_computation.9.clone.1 | convolution fusion | flops 698577408 | bytes 19771904 | tf_op jit(solution)/shard_map/while/body/eval_jaxpr/hqk,khd->qhd/dot_general | solution.py:30
  125.6 2.8 %reshape.115 = bf16[2,8,192,1,144]{2,1,4,0,3:T(8,128)(2,1)} reshape(bf16[2,1536,2,72]{1,3,2,0:T(8,128)(2,1)} %get-tuple-element.32) | data formatting | bytes 1769472 | tf_op jit(solution)/shard_map/reshape | solution.py:63
  128.5 2.5 copy.84
  131.0 4.4 %all-to-all-start.1 = ((bf16[2,8,192,1,144]{2,4,0,3,1:T(8,128)(2,1)}), bf16[2,8,192,1,144]{2,4,0,3,1:T(8,128)(2,1)}, u32[]{:S(2)}, u32[]{:S(2)}) async-start(bf16[2,8,192,1,144]{2,4,0,3,1:T(8,128)(2,1)} %copy.84), calls=%async_computation.1 | async-start | bytes 2359296 | tf_op jit(solution)/shard_map/all_to_all | solution.py:64
  136.1 15.7 %all-to-all-done.1 = bf16[2,8,192,1,144]{2,4,0,3,1:T(8,128)(2,1)} async-done(((bf16[2,8,192,1,144]{2,4,0,3,1:T(8,128)(2,1)}), bf16[2,8,192,1,144]{2,4,0,3,1:T(8,128)(2,1)}, u32[]{:S(2)}, u32[]{:S(2)}) %all-to-all-start.1) | async-done | bytes 884768 | tf_op jit(solution)/shard_map/all_to_all | solution.py:64
  151.7 1.3 copy.85
  153.1 2.5 fusion.62
  157.3 33.3 %all_to_all.51 = bf16[2,1,192,1152]{3,0,1,2:T(2,128)(2,1)S(1)} all-to-all(bf16[2,1,192,1152]{3,0,1,2:T(2,128)(2,1)S(1)} %copy.87), channel_id=1, replica_groups=mesh['frame'=32,'pos'=8] {'frame'}, dimensions={2} | all-to-all | bytes 1769472 | tf_op jit(solution)/shard_map/all_to_all | solution.py:79
  190.8 5.0 %convolution_convert_fusion = bf16[384,3456]{1,0:T(8,128)(2,1)} fusion(bf16[384,1152]{1,0:T(8,128)(2,1)S(1)} %bitcast.117, bf16[1152,3456]{1,0:T(8,128)(2,1)S(1)} %bitcast.119), kind=kOutput, calls=%fused_computation.32 | convolution fusion | flops 3058974720 | bytes 11501568 | tf_op jit(solution)/shard_map/dot_general | solution.py:80
  195.8 10.7 %reshape.117 = bf16[2,32,6,3,16,72]{5,4,3,2,1,0:T(8,128)(2,1)} reshape(bf16[384,3456]{1,0:T(8,128)(2,1)} %convolution_convert_fusion) | data formatting | bytes 5308416 | tf_op jit(solution)/shard_map/reshape | solution.py:86
  206.5 3.3 %fusion.61 = (bf16[2,32,6,1,16,72]{5,4,3,2,1,0:T(8,128)(2,1)S(1)}, bf16[2,32,6,1,16,72]{5,4,3,2,1,0:T(8,128)(2,1)S(1)}, bf16[2,32,6,1,16,72]{5,4,3,2,1,0:T(8,128)(2,1)S(1)}) fusion(bf16[2,32,6,3,16,72]{5,4,3,2,1,0:T(8,128)(2,1)} %reshape.117), kind=kLoop, calls=%fused_computation.74 | loop fusion | bytes 5308416 | tf_op jit(solution)/shard_map/slice | solution.py:94
  209.8 1.7 fusion.31
  211.6 1.8 fusion.45
  213.4 7.7 %fusion.63 = (f32[2,6,16,32]{3,2,1,0:T(8,128)S(1)}, f32[2,6,16,32,32]{3,4,2,1,0:T(8,128)S(1)}) fusion(f32[2,6,16,32,32]{3,4,2,1,0:T(8,128)S(1)} %fusion.45), kind=kOutput, calls=%fused_computation.76 | output fusion | flops 786463 | bytes 1597440 | tf_op jit(solution)/shard_map/sub | solution.py:19
  221.1 1.2 fusion.54
  222.3 1.8 copy.99
  224.0 4.3 %reshape.124 = bf16[2,32,6,1152]{3,0,2,1:T(2,128)(2,1)S(1)} reshape(bf16[2,32,6,16,72]{4,3,0,2,1:T(8,128)(2,1)} %copy.99) | data formatting | bytes 1769472 | tf_op jit(solution)/shard_map/reshape | solution.py:96
  228.4 29.5 %all_to_all.52 = bf16[2,32,6,1152]{3,0,2,1:T(2,128)(2,1)S(1)} all-to-all(bf16[2,32,6,1152]{3,0,2,1:T(2,128)(2,1)S(1)} %reshape.124), channel_id=1, replica_groups=mesh['frame'=32,'pos'=8] {'frame'}, dimensions={1} | all-to-all | bytes 1769472 | tf_op jit(solution)/shard_map/all_to_all | solution.py:97
  (38 shorter events, 5.7 us)
Async XLA Ops:
  0.0 153.1 %copy-start = (bf16[1152,1152]{1,0:T(8,128)(2,1)S(1)}, bf16[1152,1152]{1,0:T(8,128)(2,1)}, u32[]{:S(2)}) copy-start(bf16[1152,1152]{1,0:T(8,128)(2,1)} %param.16) | copy-start | bytes 7962628
  9.7 47.9 %all-to-all-start = ((bf16[2,1,192,3,8,144]{2,5,3,0,1,4:T(8,128)(2,1)}), bf16[2,1,192,3,8,144]{2,5,3,0,1,4:T(8,128)(2,1)}, u32[]{:S(2)}, u32[]{:S(2)}) async-start(bf16[2,1,192,3,8,144]{2,5,3,0,1,4:T(8,128)(2,1)} %copy.82), calls=%async_computation | async-start | bytes 7077888 | tf_op jit(solution)/shard_map/all_to_all | solution.py:58
  63.5 6.4 %copy-start.3 = (f32[72]{0:T(128)S(1)}, f32[72]{0:T(128)}, u32[]{:S(2)}) copy-start(f32[72]{0:T(128)} %param.17) | copy-start | bytes 868
  63.5 6.4 %copy-start.4 = (f32[72]{0:T(128)S(1)}, f32[72]{0:T(128)}, u32[]{:S(2)}) copy-start(f32[72]{0:T(128)} %param.18) | copy-start | bytes 868
  71.3 1.1 copy-start.1
  99.2 1.1 copy-start.1
  131.0 22.1 %copy-start.2 = (bf16[2,1,192,1152]{3,2,1,0:T(8,128)(2,1)S(1)}, bf16[2,1,192,1152]{3,2,1,0:T(8,128)(2,1)}, u32[]{:S(2)}) copy-start(bf16[2,1,192,1152]{3,2,1,0:T(8,128)(2,1)} %param.14) | copy-start | bytes 2654212
  131.0 20.8 %all-to-all-start.1 = ((bf16[2,8,192,1,144]{2,4,0,3,1:T(8,128)(2,1)}), bf16[2,8,192,1,144]{2,4,0,3,1:T(8,128)(2,1)}, u32[]{:S(2)}, u32[]{:S(2)}) async-start(bf16[2,8,192,1,144]{2,4,0,3,1:T(8,128)(2,1)} %copy.84), calls=%async_computation.1 | async-start | bytes 2359296 | tf_op jit(solution)/shard_map/all_to_all | solution.py:64
  153.1 2.9 %copy-start.5 = (f32[2,1152]{1,0:T(2,128)S(1)}, f32[2,1152]{1,0:T(2,128)}, u32[]{:S(2)}) copy-start(f32[2,1152]{1,0:T(2,128)} %param.19) | copy-start | bytes 27652
  153.1 37.6 %slice-start = ((s8[7962624]{0:T(1024)(128)(4,1)}), s8[4194304]{0:T(1024)(128)(4,1)S(1)}, s32[]{:S(2)}) async-start(s8[7962624]{0:T(1024)(128)(4,1)} %bitcast.118), calls=%async_computation.4 | async-start | bytes 8388608
  155.7 35.1 %slice-start.1 = ((s8[7962624]{0:T(1024)(128)(4,1)}), s8[3768320]{0:T(1024)(128)(4,1)S(1)}, s32[]{:S(2)}) async-start(s8[7962624]{0:T(1024)(128)(4,1)} %bitcast.118), calls=%async_computation.5 | async-start | bytes 7536640
  209.8 1.8 copy-start.6
  209.8 1.8 copy-start.7
where the time goes:
time: 263 us; the launch traced here: 259 us
  blocking collectives  62.9 us (24%)
  matrix products  61.2 us (23%)
  waiting for transfers between devices  57.4 us (22%)
  local copies, waits for them, and re-layouts  55.3 us (21%)
  other arithmetic  11.3 us (4%)
  starting transfers between devices  10.6 us (4%)
    all_to_all x1, waiting for transfers between devices, per_device(): lax.all_to_all(packed, 'pos', split_axis=4, concat_axis=1, tiled=True)  41.8 us
    all_to_all x1, blocking collectives, per_device(): lax.all_to_all(normed, 'frame', split_axis=2, concat_axis=1, tiled=True)  33.3 us
    all_to_all x1, blocking collectives, per_device(): lax.all_to_all(result, 'frame', split_axis=1, concat_axis=2, tiled=True)  29.5 us
    dot_general x2, matrix products, spatial_attend(): jnp.einsum('hqk,khd->qhd', weights, element[:, 2], preferred_element_type...  20.8 us
    dot_general x2, matrix products, spatial_attend(): jnp.einsum('qhd,khd->hqk', query_norm, keys_norm, preferred_element_type=...  15.9 us
    all_to_all x1, waiting for transfers between devices, per_device(): lax.all_to_all(outgoing, 'pos', split_axis=1, concat_axis=3, tiled=True)  15.7 us
    sub x2, matrix products, softmax_weights(): expons = jnp.exp(scores - row_top)  14 us
    reshape x1, local copies, waits for them, and re-layouts, per_device(): by_frames.reshape(videos, frames_all, pos_group, 3, heads, head_dim)  10.7 us
  transfers between devices with their start and end apart: 2, of which 2 were waited for; matrix products, arithmetic and copies ran while one was open for 0% of the time, Pallas kernels for 0%

commit v1 on v0

v1 whole, which is shorter than its diff:
```python
import math

import jax
import jax.numpy as jnp
from jax import lax
from jax.experimental import pallas as pl
from jax.experimental.pallas import tpu as pltpu
from jax.sharding import PartitionSpec as P

EPSILON = 1e-06
MESH = pl.DeviceIdType.MESH
BF16 = jnp.bfloat16
F32 = jnp.float32
HEAD_DIM = 72
LANES = 128
SLAB = 4
LOG2E = 1.4426950408889634
SCORE_SCALE = LOG2E / math.sqrt(HEAD_DIM)


def norm_rows(values, gain):
    mean = jnp.sum(values * values, axis=0, keepdims=True) * (1.0 / HEAD_DIM)
    return values * lax.rsqrt(mean + EPSILON) * gain


def spatial_kernel(
    x_ref,
    residual_ref,
    gate_ref,
    proj_ref,
    qgain_ref,
    kgain_ref,
    shift_ref,
    scale_ref,
    out_ref,
    wide,
    send,
    recv,
    queries,
    keys,
    values,
    scores,
    outgoing,
    attended,
    send_sem,
    recv_sem,
    back_send_sem,
    back_recv_sem,
):
    me = lax.axis_index("pos")
    odd = lax.rem(me, 2)
    barrier = pltpu.get_barrier_semaphore()
    for r in range(1, 8):
        pl.semaphore_signal(
            barrier, inc=1, device_id={"pos": lax.rem(me + r, 8)}, device_id_type=MESH
        )

    swap = jnp.zeros((64, LANES), jnp.int32) + odd == 1

    def turn(j, carry):
        columns = pl.ds(pl.multiple_of(j * LANES, LANES), LANES)
        for t in range(3):
            first = x_ref[0, t, :, columns].astype(F32)
            second = x_ref[1, t, :, columns].astype(F32)
            low, high = first[128:], second[:64]
            block = jnp.concatenate(
                [first[:128], jnp.where(swap, high, low), jnp.where(swap, low, high), second[64:]],
                axis=0,
            )
            wide[t, columns, :] = block.T
        return carry

    lax.fori_loop(0, 9, turn, 0)

    def exchange(h, r):
        peer = lax.rem(me + r, 8)
        return pltpu.make_async_remote_copy(
            src_ref=send.at[2 * peer + h],
            dst_ref=recv.at[h, r],
            send_sem=send_sem.at[h, r],
            recv_sem=recv_sem.at[h, r],
            device_id={"pos": peer},
            device_id_type=MESH,
        )

    for h in range(2):

        def pack(d, carry):
            rows = pl.ds(pl.multiple_of(d * 144 + 72 * h, 8), HEAD_DIM)
            send[2 * d + h, 0] = norm_rows(wide[0, rows, :], qgain_ref[...]).astype(BF16)
            send[2 * d + h, 1] = norm_rows(wide[1, rows, :], kgain_ref[...]).astype(BF16)
            send[2 * d + h, 2] = wide[2, rows, :].astype(BF16)
            return carry

        lax.fori_loop(0, 8, pack, 0)
        if h == 0:
            pl.semaphore_wait(barrier, 7)
        for r in range(1, 8):
            exchange(h, r).start()
    for h in range(2):
        recv[h, 0] = send[2 * me + h]
    for v in range(2):
        values[v, 72:80, :] = jnp.ones((8, 1536), BF16)

    lane = lax.broadcasted_iota(jnp.int32, (HEAD_DIM, LANES), 1)
    straight = (lane < 64) == ((jnp.zeros((HEAD_DIM, LANES), jnp.int32) + odd) == 0)

    def give_back(h, r):
        return pltpu.make_async_remote_copy(
            src_ref=outgoing.at[h, r],
            dst_ref=attended.at[2 * me + h],
            send_sem=back_send_sem.at[h, r],
            recv_sem=back_recv_sem.at[h, r],
            device_id={"pos": lax.rem(me + 8 - r, 8)},
            device_id_type=MESH,
        )

    for h in range(2):
        for i in range(4):
            for r in (2 * i, 2 * i + 1):
                if r > 0:
                    exchange(h, r).wait_recv()
            span = slice(384 * i, 384 * i + 384)
            for t in range(3):
                a, b = recv[h, 2 * i, t], recv[h, 2 * i + 1, t]
                amid, bmid = a[:, 128:256].astype(F32), b[:, 128:256].astype(F32)
                mids = (
                    jnp.where(straight, amid, bmid).astype(BF16),
                    jnp.where(straight, bmid, amid).astype(BF16),
                )
                for v in range(2):
                    edge = slice(256 * v, 256 * v + 128)
                    pieces = (a[:, edge], b[:, edge], mids[v])
                    for n, piece in enumerate(pieces):
                        place = slice(384 * i + 128 * n, 384 * i + 128 * n + 128)
                        if t == 0:
                            queries[v, :, place] = piece
                        elif t == 1:
                            keys[v, place, :] = piece.T
                        else:
                            values[v, 0:72, place] = piece
        for g in range(2):
            results = []
            for v in range(2):
                block = queries[v, :, 768 * g : 768 * g + 768]
                top = None
                for c in range(6):
                    part = jnp.dot(
                        keys[v, 256 * c : 256 * c + 256, :], block, preferred_element_type=F32
                    )
                    scores[v, 256 * c : 256 * c + 256, :] = part
                    part_top = jnp.max(part.reshape(32, 8, 768), axis=0)
                    top = part_top if top is None else jnp.maximum(top, part_top)
                top = jnp.max(top, axis=0, keepdims=True) * SCORE_SCALE
                total = None
                for c in range(6):
                    expons = jnp.exp2(
                        scores[v, 256 * c : 256 * c + 256, :] * SCORE_SCALE - top
                    ).astype(BF16)
                    part = jnp.dot(
                        values[v, :, 256 * c : 256 * c + 256], expons, preferred_element_type=F32
                    )
                    total = part if total is None else total + part
                results.append(total[:72] / total[72:73])
            for i in (2 * g, 2 * g + 1):
                base = 384 * (i - 2 * g)
                mid0 = results[0][:, base + 256 : base + 384]
                mid1 = results[1][:, base + 256 : base + 384]
                for n in range(2):
                    r = 2 * i + n
                    edge = slice(base + 128 * n, base + 128 * n + 128)
                    if n == 0:
                        mid = jnp.where(straight, mid0, mid1)
                    else:
                        mid = jnp.where(straight, mid1, mid0)
                    pieces = (results[0][:, edge], mid, results[1][:, edge])
                    for m, piece in enumerate(pieces):
                        place = slice(128 * m, 128 * m + 128)
                        if r == 0:
                            attended[2 * me + h, :, place] = piece.astype(BF16)
                        else:
                            outgoing[h, r, :, place] = piece.astype(BF16)
                    if r > 0:
                        give_back(h, r).start()

    def arrived(h, r):
        return pltpu.make_async_remote_copy(
            src_ref=outgoing.at[h, r],
            dst_ref=attended.at[2 * lax.rem(me + r, 8) + h],
            send_sem=back_send_sem.at[h, r],
            recv_sem=back_recv_sem.at[h, r],
            device_id={"pos": lax.rem(me + r, 8)},
            device_id_type=MESH,
        )

    for h in range(2):
        for r in range(1, 8):
            arrived(h, r).wait_recv()
    for n in range(16):
        wide[0, 72 * n : 72 * n + 72, :] = attended[n].astype(F32)
    gate_odd = jnp.zeros((LANES, 1152), jnp.int32) + odd == 1
    for tile in range(3):
        rows = wide[0, :, 128 * tile : 128 * tile + 128].T
        if tile == 1:
            rows = jnp.where(gate_odd, jnp.concatenate([rows[64:], rows[:64]], axis=0), rows)
        mixed = jnp.dot(rows.astype(BF16), proj_ref[...], preferred_element_type=F32)
        for half in range(2):
            start = 128 * tile + 64 * half
            v, p = divmod(start, 192)
            updated = (
                residual_ref[v, p : p + 64, :].astype(F32)
                + gate_ref[v : v + 1, :] * mixed[64 * half : 64 * half + 64]
            ).astype(BF16)
            widened = updated.astype(F32)
            centred = widened - jnp.mean(widened, axis=-1, keepdims=True)
            spread = jnp.mean(centred * centred, axis=-1, keepdims=True)
            scaled = centred * lax.rsqrt(spread + EPSILON) * (1.0 + scale_ref[v : v + 1, :])
            normed = (scaled + shift_ref[v : v + 1, :]).astype(BF16)
            out_ref[start // SLAB : start // SLAB + 16] = normed.reshape(16, SLAB, 1152)
    for h in range(2):
        for r in range(1, 8):
            exchange(h, r).wait_send()
            give_back(h, r).wait_send()


def temporal_kernel(
    rows_ref,
    weight_ref,
    qgain_ref,
    kgain_ref,
    out_ref,
    weight,
    recv,
    turned,
    result,
    outgoing,
    back,
    weight_sem,
    send_sem,
    recv_sem,
    back_send_sem,
    back_recv_sem,
):
    me = lax.axis_index("frame")
    load = pltpu.make_async_copy(weight_ref, weight, weight_sem)
    load.start()
    barrier = pltpu.get_barrier_semaphore()

    def greet(r, carry):
        pl.semaphore_signal(
            barrier, inc=1, device_id={"frame": lax.rem(me + r, 32)}, device_id_type=MESH
        )
        return carry

    lax.fori_loop(1, 32, greet, 0)
    pl.semaphore_wait(barrier, 31)

    for i in range(3):

        def give(r, carry):
            peer = lax.rem(me + r, 32)
            pltpu.make_async_remote_copy(
                src_ref=rows_ref.at[3 * peer + i],
                dst_ref=recv.at[i, r],
                send_sem=send_sem.at[i],
                recv_sem=recv_sem.at[i],
                device_id={"frame": peer},
                device_id_type=MESH,
            ).start()
            return carry

        lax.fori_loop(1, 32, give, 0)
        recv[i, 0] = rows_ref[3 * me + i]

    def all_of(buffer, i, send_sems, recv_sems):
        return pltpu.make_async_remote_copy(
            src_ref=buffer.at[i, pl.ds(1, 31)],
            dst_ref=buffer.at[i, pl.ds(1, 31)],
            send_sem=send_sems.at[i],
            recv_sem=recv_sems.at[i],
            device_id={"frame": lax.rem(me + 1, 32)},
            device_id_type=MESH,
        )

    load.wait()
    row = lax.broadcasted_iota(jnp.int32, (LANES, LANES), 0)
    column = lax.broadcasted_iota(jnp.int32, (LANES, LANES), 1)
    same = lax.rem(row, SLAB) == lax.rem(column, SLAB)
    for i in range(3):
        all_of(recv, i, send_sem, recv_sem).wait_recv()
        tokens = recv[i].reshape(LANES, 1152)
        for t in range(3):
            projected = jnp.dot(
                tokens, weight[:, 1152 * t : 1152 * t + 1152], preferred_element_type=F32
            ).astype(BF16)
            turned[t] = projected.astype(F32).T
        for n in range(16):
            head = slice(72 * n, 72 * n + 72)
            query = norm_rows(turned[0, head, :], qgain_ref[...]).astype(BF16)
            key = norm_rows(turned[1, head, :], kgain_ref[...]).astype(BF16)
            score = lax.dot_general(
                key, query, (((0,), (0,)), ((), ())), preferred_element_type=F32
            )
            score = jnp.where(same, score * SCORE_SCALE, -1e30)
            expons = jnp.exp2(score - jnp.max(score, axis=0, keepdims=True))
            share = (expons / jnp.sum(expons, axis=0, keepdims=True)).astype(BF16)
            result[head, :] = jnp.dot(
                turned[2, head, :].astype(BF16), share, preferred_element_type=F32
            )
        outgoing[i] = result[...].T.astype(BF16).reshape(32, SLAB, 1152)

        def give_back(r, carry):
            pltpu.make_async_remote_copy(
                src_ref=outgoing.at[i, r],
                dst_ref=back.at[i, r],
                send_sem=back_send_sem.at[i],
                recv_sem=back_recv_sem.at[i],
                device_id={"frame": lax.rem(me + 32 - r, 32)},
                device_id_type=MESH,
            ).start()
            return carry

        lax.fori_loop(1, 32, give_back, 0)
        out_ref[3 * me + i] = outgoing[i, 0]
    for i in range(3):
        all_of(back, i, back_send_sem, back_recv_sem).wait_recv()

        def place(r, carry):
            out_ref[3 * lax.rem(me + r, 32) + i] = back[i, r]
            return carry

        lax.fori_loop(1, 32, place, 0)
    for i in range(3):
        all_of(recv, i, send_sem, recv_sem).wait_send()
        all_of(back, i, back_send_sem, back_recv_sem).wait_send()


def per_device(
    spatial_qkv,
    residual,
    spatial_gate,
    spatial_proj,
    spatial_qgain,
    spatial_kgain,
    temporal_shift,
    temporal_scale,
    temporal_qkv,
    temporal_qgain,
    temporal_kgain,
):
    vmem = pl.BlockSpec(memory_space=pltpu.VMEM)
    dma = pltpu.SemaphoreType.DMA
    split = jnp.transpose(spatial_qkv, (0, 1, 3, 2, 4)).reshape(2, 3, 192, 1152)
    modulated = pl.pallas_call(
        spatial_kernel,
        out_shape=jax.ShapeDtypeStruct((96, SLAB, 1152), BF16),
        in_specs=[vmem] * 8,
        out_specs=vmem,
        scratch_shapes=[
            pltpu.VMEM((3, 1152, 384), F32),
            pltpu.VMEM((16, 3, 72, 384), BF16),
            pltpu.VMEM((2, 8, 3, 72, 384), BF16),
            pltpu.VMEM((2, 72, 1536), BF16),
            pltpu.VMEM((2, 1536, 72), BF16),
            pltpu.VMEM((2, 80, 1536), BF16),
            pltpu.VMEM((2, 1536, 768), F32),
            pltpu.VMEM((2, 8, 72, 384), BF16),
            pltpu.VMEM((16, 72, 384), BF16),
            dma((2, 8)),
            dma((2, 8)),
            dma((2, 8)),
            dma((2, 8)),
        ],
        compiler_params=pltpu.CompilerParams(
            collective_id=0, has_side_effects=True, vmem_limit_bytes=56 * 1024 * 1024
        ),
        name="spatial",
    )(
        split,
        residual.reshape(2, 192, 1152),
        spatial_gate,
        spatial_proj,
        spatial_qgain.reshape(72, 1),
        spatial_kgain.reshape(72, 1),
        temporal_shift,
        temporal_scale,
    )
    result = pl.pallas_call(
        temporal_kernel,
        out_shape=jax.ShapeDtypeStruct((96, SLAB, 1152), BF16),
        in_specs=[vmem, pl.BlockSpec(memory_space=pl.ANY), vmem, vmem],
        out_specs=vmem,
        scratch_shapes=[
            pltpu.VMEM((1152, 3456), BF16),
            pltpu.VMEM((3, 32, SLAB, 1152), BF16),
            pltpu.VMEM((3, 1152, LANES), F32),
            pltpu.VMEM((1152, LANES), F32),
            pltpu.VMEM((3, 32, SLAB, 1152), BF16),
            pltpu.VMEM((3, 32, SLAB, 1152), BF16),
            dma,
            dma((3,)),
            dma((3,)),
            dma((3,)),
            dma((3,)),
        ],
        compiler_params=pltpu.CompilerParams(
            collective_id=1, has_side_effects=True, vmem_limit_bytes=56 * 1024 * 1024
        ),
        name="temporal",
    )(modulated, temporal_qkv, temporal_qgain.reshape(72, 1), temporal_kgain.reshape(72, 1))
    return result.reshape(2, 1, 192, 1152)


def solution(mesh):
    return jax.shard_map(
        per_device,
        mesh=mesh,
        in_specs=(
            P(None, "frame", "pos", None, None),
            P(None, "frame", "pos", None),
            P(),
            P(),
            P(),
            P(),
            P(),
            P(),
            P(),
            P(),
            P(),
        ),
        out_specs=P(None, "frame", "pos", None),
        check_vma=False,
    )
```

time: 263 us -> 123 us (0.47); the launches traced: 259 us -> 122 us
  Pallas kernels: 0 us -> 115 us
  blocking collectives: 62.9 us -> 0 us
  matrix products: 61.2 us -> 0 us
  waiting for transfers between devices: 57.4 us -> 0 us
  local copies, waits for them, and re-layouts: 55.3 us -> 7.79 us
  other arithmetic: 11.3 us -> 0 us
  starting transfers between devices: 10.6 us -> 0 us
    pallas_call x0 -> x2, Pallas kernels: none -> 115 us  [the longest x1 58.6 us: per_device(): pl.pallas_call(spatial_kernel, out_shape=jax.ShapeDtypeStruct((96, SLAB,...]
    all_to_all x2 -> x0, blocking collectives: 62.9 us -> none  [the longest x1 33.3 us: per_device(): lax.all_to_all(normed, 'frame', split_axis=2, concat_axis=1, tiled=True)]
    all_to_all x2 -> x0, waiting for transfers between devices: 57.4 us -> none  [the longest x1 41.8 us: per_device(): lax.all_to_all(packed, 'pos', split_axis=4, concat_axis=1, tiled=True)]
    dot_general x8 -> x0, matrix products: 47.2 us -> none  [the longest x2 20.8 us: spatial_attend(): jnp.einsum('hqk,khd->qhd', weights, element[:, 2], preferred_element_type...]
    reshape x7 -> x5, local copies, waits for them, and re-layouts: 32.7 us -> 7.79 us  [the longest x1 2.36 us: per_device(): return result.reshape(2, 1, 192, 1152)]
    sub x2 -> x0, matrix products: 14 us -> none  [softmax_weights(): expons = jnp.exp(scores - row_top)]
    all_to_all x2 -> x0, starting transfers between devices: 10.6 us -> none  [the longest x1 6.19 us: per_device(): lax.all_to_all(packed, 'pos', split_axis=4, concat_axis=1, tiled=True)]
    all_to_all x4 -> x0, local copies, waits for them, and re-layouts: 8.25 us -> none  [the longest x1 5.81 us: per_device(): lax.all_to_all(packed, 'pos', split_axis=4, concat_axis=1, tiled=True)]
  transfers between devices with their start and end apart: 2 -> 0, of which waited for: 2 -> 0; matrix products, arithmetic and copies ran while one was open for 0% -> 0% of each run, Pallas kernels for 0% -> 0%
where the time goes in v1:
time: 123 us; the launch traced here: 122 us
  Pallas kernels  115 us (93%)
  local copies, waits for them, and re-layouts  7.79 us (6%)
    pallas_call x1, Pallas kernels, per_device(): pl.pallas_call(spatial_kernel, out_shape=jax.ShapeDtypeStruct((96, SLAB,...  58.6 us
    pallas_call x1, Pallas kernels, per_device(): pl.pallas_call(temporal_kernel, out_shape=jax.ShapeDtypeStruct((96, SLAB,...  56 us

profile of v1, /device:TPU:1, one launch (start us, length us, event | category | flops | bytes accessed | tf_op | source)
XLA Modules:
  0.0 122.4 jit_solution(1307636421094717839)
XLA Ops:
  0.0 1.4 %copy.13.qgain_ref = f32[72,1]{1,0:T(8,128)} copy(f32[72,1]{0,1:T(1,128)} %bitcast.13) | data formatting | bytes 576 | tf_op jit(solution)/shard_map/reshape | solution.py:383
  1.4 1.4 %copy.14.kgain_ref = f32[72,1]{1,0:T(8,128)} copy(f32[72,1]{0,1:T(1,128)} %bitcast.14) | data formatting | bytes 576 | tf_op jit(solution)/shard_map/reshape | solution.py:384
  2.7 1.4 %copy.15.qgain_ref = f32[72,1]{1,0:T(8,128)} copy(f32[72,1]{0,1:T(1,128)} %bitcast.15) | data formatting | bytes 576 | tf_op jit(solution)/shard_map/reshape | solution.py:410
  4.1 1.4 %copy.16.kgain_ref = f32[72,1]{1,0:T(8,128)} copy(f32[72,1]{0,1:T(1,128)} %bitcast.16) | data formatting | bytes 576 | tf_op jit(solution)/shard_map/reshape | solution.py:410
  5.4 58.6 %spatial.1.rows_ref = bf16[96,4,1152]{2,1,0:T(4,128)(2,1)} custom-call(bf16[2,3,192,1152]{3,2,1,0:T(8,128)(2,1)} %bitcast.11, bf16[2,192,1152]{2,1,0:T(8,128)(2,1)} %bitcast.12, f32[2,1152]{1,0:T(2,128)} %gate_ref.1, bf16[1152,1152]{1,0:T(8,128)(2,1)} %proj_ref.1, f32[72,1]{1,0:T(8,128)} %copy.13.qgain_ref, f32[72,1]{1,0:T(8,128)} %copy.14.kgain_ref, ...), custom_call_target="tpu_custom_call" | custom-call | tf_op jit(solution)/shard_map/spatial/pallas_call | solution.py:354
  64.0 56.0 %temporal.1 = bf16[96,4,1152]{2,1,0:T(4,128)(2,1)} custom-call(bf16[96,4,1152]{2,1,0:T(4,128)(2,1)} %spatial.1.rows_ref, bf16[1152,3456]{1,0:T(8,128)(2,1)} %weight_ref.1, f32[72,1]{1,0:T(8,128)} %copy.15.qgain_ref, f32[72,1]{1,0:T(8,128)} %copy.16.kgain_ref), custom_call_target="tpu_custom_call" | custom-call | tf_op jit(solution)/shard_map/temporal/pallas_call | solution.py:388
  120.0 2.4 %reshape.27 = bf16[2,1,192,1152]{3,2,0,1:T(8,128)(2,1)} reshape(bf16[96,4,1152]{2,1,0:T(4,128)(2,1)} %temporal.1) | data formatting | bytes 1769472 | tf_op jit(solution)/shard_map/reshape | solution.py:411

commit v2 on v1

v2 whole, which is shorter than its diff:
```python
import math

import jax
import jax.numpy as jnp
from jax import lax
from jax.experimental import pallas as pl
from jax.experimental.pallas import tpu as pltpu
from jax.sharding import PartitionSpec as P

EPSILON = 1e-06
MESH = pl.DeviceIdType.MESH
BF16 = jnp.bfloat16
F32 = jnp.float32
HEAD_DIM = 72
LANES = 128
SLAB = 4
LOG2E = 1.4426950408889634
SCORE_SCALE = LOG2E / math.sqrt(HEAD_DIM)


def norm_rows(values, gain):
    mean = jnp.sum(values * values, axis=0, keepdims=True) * (1.0 / HEAD_DIM)
    return values * lax.rsqrt(mean + EPSILON) * gain


def fused_kernel(
    x_ref,
    residual_ref,
    proj_ref,
    weight_ref,
    gate_ref,
    shift_ref,
    scale_ref,
    spatial_qgain_ref,
    spatial_kgain_ref,
    temporal_qgain_ref,
    temporal_kgain_ref,
    out_ref,
    taken,
    residual,
    proj,
    weight,
    gains,
    wide,
    send,
    recv,
    queries,
    keys,
    values,
    scores,
    outgoing,
    attended,
    slabs,
    slab_recv,
    turned,
    result,
    slab_outgoing,
    slab_back,
    load_sem,
    take_sem,
    send_sem,
    recv_sem,
    back_send_sem,
    back_recv_sem,
    slab_send_sem,
    slab_recv_sem,
    slab_back_send_sem,
    slab_back_recv_sem,
):
    me = lax.axis_index("pos")
    frame = lax.axis_index("frame")
    odd = lax.rem(me, 2)

    def take(s):
        j = lax.rem(me + 1 + s, 9)
        columns = pl.ds(pl.multiple_of(j * LANES, LANES), LANES)
        return pltpu.make_async_copy(
            x_ref.at[:, :, :, columns], taken.at[s], take_sem.at[s]
        )

    for s in range(9):
        take(s).start()
    barrier = pltpu.get_barrier_semaphore()
    for r in range(1, 8):
        pl.semaphore_signal(
            barrier, inc=1, device_id={"pos": lax.rem(me + r, 8)}, device_id_type=MESH
        )

    def greet(r, carry):
        pl.semaphore_signal(
            barrier, inc=1, device_id={"frame": lax.rem(frame + r, 32)}, device_id_type=MESH
        )
        return carry

    lax.fori_loop(1, 32, greet, 0)
    loads = [
        pltpu.make_async_copy(source, target, load_sem.at[n])
        for n, (source, target) in enumerate(
            ((residual_ref, residual), (proj_ref, proj), (weight_ref, weight))
        )
    ]
    for load in loads:
        load.start()
    for n, gain_ref in enumerate(
        (spatial_qgain_ref, spatial_kgain_ref, temporal_qgain_ref, temporal_kgain_ref)
    ):
        column = jnp.broadcast_to(gain_ref[...], (LANES, HEAD_DIM)).T
        for m in range(3):
            gains[n, :, 128 * m : 128 * m + 128] = column

    swap = jnp.zeros((64, LANES), jnp.int32) + odd == 1

    def turn(s):
        j = lax.rem(me + 1 + s, 9)
        rows = pl.ds(pl.multiple_of(j * LANES, LANES), LANES)
        for t in range(3):
            first = taken[s, 0, t].astype(F32)
            second = taken[s, 1, t].astype(F32)
            low, high = first[128:], second[:64]
            block = jnp.concatenate(
                [first[:128], jnp.where(swap, high, low), jnp.where(swap, low, high), second[64:]],
                axis=0,
            )
            wide[t, rows, :] = block.T

    def pack(d, h):
        rows = pl.ds(pl.multiple_of(d * 144 + 72 * h, 8), HEAD_DIM)
        send[2 * d + h, 0] = norm_rows(wide[0, rows, :], gains[0]).astype(BF16)
        send[2 * d + h, 1] = norm_rows(wide[1, rows, :], gains[1]).astype(BF16)
        send[2 * d + h, 2] = wide[2, rows, :].astype(BF16)

    def exchange(stage, peer, r):
        h = 0 if stage == 0 else 1
        part = ((0, 3), (1, 2), (0, 1))[stage]
        return pltpu.make_async_remote_copy(
            src_ref=send.at[2 * peer + h, pl.ds(*part)],
            dst_ref=recv.at[h, r, pl.ds(*part)],
            send_sem=send_sem.at[stage, r],
            recv_sem=recv_sem.at[stage, r],
            device_id={"pos": peer},
            device_id_type=MESH,
        )

    take(0).wait()
    turn(0)
    take(1).wait()
    turn(1)
    pl.semaphore_wait(barrier, 38)

    def feed(s, carry):
        @pl.when(s > 1)
        def _():
            take(s).wait()
            turn(s)

        j = lax.rem(me + 1 + s, 9)

        @pl.when(j >= 1)
        def _():
            peer = j - 1
            pack(peer, 0)
            exchange(0, peer, lax.rem(peer + 8 - me, 8)).start()

        return carry

    lax.fori_loop(1, 9, feed, 0)

    def feed_second(r, carry):
        peer = lax.rem(me + r, 8)
        pack(peer, 1)
        exchange(1, peer, r).start()
        return carry

    lax.fori_loop(1, 8, feed_second, 0)
    for r in range(1, 8):
        exchange(2, lax.rem(me + r, 8), r).start()
    for h in range(2):
        pack(me, h)
        recv[h, 0] = send[2 * me + h]
    for v in range(2):
        values[v, 72:80, :] = jnp.ones((8, 1536), BF16)

    lane = lax.broadcasted_iota(jnp.int32, (HEAD_DIM, LANES), 1)
    straight = (lane < 64) == ((jnp.zeros((HEAD_DIM, LANES), jnp.int32) + odd) == 0)

    def give_back(h, r):
        return pltpu.make_async_remote_copy(
            src_ref=outgoing.at[h, r],
            dst_ref=attended.at[2 * me + h],
            send_sem=back_send_sem.at[h, r],
            recv_sem=back_recv_sem.at[h, r],
            device_id={"pos": lax.rem(me + 8 - r, 8)},
            device_id_type=MESH,
        )

    def await_pair(stage, i):
        for r in (2 * i, 2 * i + 1):
            if r > 0:
                exchange(stage, lax.rem(me + r, 8), r).wait_recv()

    def spread(h, i, t):
        a, b = recv[h, 2 * i, t], recv[h, 2 * i + 1, t]
        amid, bmid = a[:, 128:256].astype(F32), b[:, 128:256].astype(F32)
        mids = (
            jnp.where(straight, amid, bmid).astype(BF16),
            jnp.where(straight, bmid, amid).astype(BF16),
        )
        for v in range(2):
            edge = slice(256 * v, 256 * v + 128)
            for n, piece in enumerate((a[:, edge], b[:, edge], mids[v])):
                place = slice(384 * i + 128 * n, 384 * i + 128 * n + 128)
                if t == 0:
                    queries[v, :, place] = piece
                elif t == 1:
                    keys[v, place, :] = piece.T
                else:
                    values[v, 0:72, place] = piece

    for h in range(2):
        for i in range(4):
            await_pair(h, i)
            spread(h, i, 1)
            spread(h, i, 2)
        for g in range(2):
            for i in (2 * g, 2 * g + 1):
                if h == 1:
                    await_pair(2, i)
                spread(h, i, 0)
            results = []
            for v in range(2):
                block = queries[v, :, 768 * g : 768 * g + 768]
                top = None
                for c in range(6):
                    part = jnp.dot(
                        keys[v, 256 * c : 256 * c + 256, :], block, preferred_element_type=F32
                    )
                    scores[v, 256 * c : 256 * c + 256, :] = part
                    part_top = jnp.max(part.reshape(32, 8, 768), axis=0)
                    top = part_top if top is None else jnp.maximum(top, part_top)
                top = jnp.max(top, axis=0, keepdims=True) * SCORE_SCALE
                total = None
                for c in range(6):
                    expons = jnp.exp2(
                        scores[v, 256 * c : 256 * c + 256, :] * SCORE_SCALE - top
                    ).astype(BF16)
                    part = jnp.dot(
                        values[v, :, 256 * c : 256 * c + 256], expons, preferred_element_type=F32
                    )
                    total = part if total is None else total + part
                results.append(total[:72] / total[72:73])
            for i in (2 * g, 2 * g + 1):
                base = 384 * (i - 2 * g)
                mid0 = results[0][:, base + 256 : base + 384]
                mid1 = results[1][:, base + 256 : base + 384]
                for n in range(2):
                    r = 2 * i + n
                    edge = slice(base + 128 * n, base + 128 * n + 128)
                    if n == 0:
                        mid = jnp.where(straight, mid0, mid1)
                    else:
                        mid = jnp.where(straight, mid1, mid0)
                    pieces = (results[0][:, edge], mid, results[1][:, edge])
                    for m, piece in enumerate(pieces):
                        place = slice(128 * m, 128 * m + 128)
                        if r == 0:
                            attended[2 * me + h, :, place] = piece.astype(BF16)
                        else:
                            outgoing[h, r, :, place] = piece.astype(BF16)
                    if r > 0:
                        give_back(h, r).start()

    def arrived(h, r):
        return pltpu.make_async_remote_copy(
            src_ref=outgoing.at[h, r],
            dst_ref=attended.at[2 * lax.rem(me + r, 8) + h],
            send_sem=back_send_sem.at[h, r],
            recv_sem=back_recv_sem.at[h, r],
            device_id={"pos": lax.rem(me + r, 8)},
            device_id_type=MESH,
        )

    for load in loads:
        load.wait()
    for h in range(2):
        for r in range(1, 8):
            arrived(h, r).wait_recv()
    for n in range(16):
        wide[0, 72 * n : 72 * n + 72, :] = attended[n].astype(F32)
    swap_rows = jnp.zeros((LANES, 1152), jnp.int32) + odd == 1

    def give_slab(i, r):
        peer = lax.rem(frame + r, 32)
        return pltpu.make_async_remote_copy(
            src_ref=slabs.at[32 * i + peer],
            dst_ref=slab_recv.at[i, r],
            send_sem=slab_send_sem.at[i],
            recv_sem=slab_recv_sem.at[i],
            device_id={"frame": peer},
            device_id_type=MESH,
        )

    for tile in range(3):
        rows = wide[0, :, 128 * tile : 128 * tile + 128].T
        if tile == 1:
            rows = jnp.where(swap_rows, jnp.concatenate([rows[64:], rows[:64]], axis=0), rows)
        mixed = jnp.dot(rows.astype(BF16), proj[...], preferred_element_type=F32)
        for half in range(2):
            start = 128 * tile + 64 * half
            v, p = divmod(start, 192)
            updated = (
                residual[v, p : p + 64, :].astype(F32)
                + gate_ref[v : v + 1, :] * mixed[64 * half : 64 * half + 64]
            ).astype(BF16)
            widened = updated.astype(F32)
            centred = widened - jnp.mean(widened, axis=-1, keepdims=True)
            spread_of = jnp.mean(centred * centred, axis=-1, keepdims=True)
            scaled = centred * lax.rsqrt(spread_of + EPSILON) * (1.0 + scale_ref[v : v + 1, :])
            normed = (scaled + shift_ref[v : v + 1, :]).astype(BF16)
            slabs[start // SLAB : start // SLAB + 16] = normed.reshape(16, SLAB, 1152)

        def give(r, carry):
            give_slab(tile, r).start()
            return carry

        lax.fori_loop(1, 32, give, 0)
        slab_recv[tile, 0] = slabs[32 * tile + frame]

    def all_of(buffer, send_sem, recv_sem):
        return pltpu.make_async_remote_copy(
            src_ref=buffer,
            dst_ref=buffer,
            send_sem=send_sem,
            recv_sem=recv_sem,
            device_id={"frame": lax.rem(frame + 1, 32)},
            device_id_type=MESH,
        )

    row = lax.broadcasted_iota(jnp.int32, (LANES, LANES), 0)
    column = lax.broadcasted_iota(jnp.int32, (LANES, LANES), 1)
    same = lax.rem(row, SLAB) == lax.rem(column, SLAB)
    for i in range(3):
        all_of(
            slab_recv.at[i, pl.ds(1, 31)], slab_send_sem.at[i], slab_recv_sem.at[i]
        ).wait_recv()
        tokens = slab_recv[i].reshape(LANES, 1152)
        for t in range(3):
            projected = jnp.dot(
                tokens, weight[:, 1152 * t : 1152 * t + 1152], preferred_element_type=F32
            ).astype(BF16)
            turned[t] = projected.astype(F32).T
        for n in range(16):
            head = slice(72 * n, 72 * n + 72)
            query = norm_rows(turned[0, head, :], gains[2, :, 0:128]).astype(BF16)
            key = norm_rows(turned[1, head, :], gains[3, :, 0:128]).astype(BF16)
            score = lax.dot_general(
                key, query, (((0,), (0,)), ((), ())), preferred_element_type=F32
            )
            score = jnp.where(same, score * SCORE_SCALE, -1e30)
            expons = jnp.exp2(score - jnp.max(score, axis=0, keepdims=True))
            share = (expons / jnp.sum(expons, axis=0, keepdims=True)).astype(BF16)
            result[head, :] = jnp.dot(
                turned[2, head, :].astype(BF16), share, preferred_element_type=F32
            )
        slab_outgoing[i] = result[...].T.astype(BF16).reshape(32, SLAB, 1152)

        def return_slab(r, carry):
            pltpu.make_async_remote_copy(
                src_ref=slab_outgoing.at[i, r],
                dst_ref=slab_back.at[32 * i + frame],
                send_sem=slab_back_send_sem.at[i],
                recv_sem=slab_back_recv_sem.at[i],
                device_id={"frame": lax.rem(frame + 32 - r, 32)},
                device_id_type=MESH,
            ).start()
            return carry

        lax.fori_loop(1, 32, return_slab, 0)
        slab_back[32 * i + frame] = slab_outgoing[i, 0]
    for stage in range(3):
        for r in range(1, 8):
            exchange(stage, lax.rem(me + r, 8), r).wait_send()
    for h in range(2):
        for r in range(1, 8):
            give_back(h, r).wait_send()
    for i in range(3):
        all_of(
            slab_back.at[pl.ds(32 * i, 31)], slab_back_send_sem.at[i], slab_back_recv_sem.at[i]
        ).wait_recv()
        out_ref[128 * i : 128 * i + 128, :] = slab_back[32 * i : 32 * i + 32].reshape(128, 1152)
    for i in range(3):
        all_of(
            slab_recv.at[i, pl.ds(1, 31)], slab_send_sem.at[i], slab_recv_sem.at[i]
        ).wait_send()
        all_of(
            slab_back.at[pl.ds(32 * i, 31)], slab_back_send_sem.at[i], slab_back_recv_sem.at[i]
        ).wait_send()


def per_device(
    spatial_qkv,
    residual,
    spatial_gate,
    spatial_proj,
    spatial_qgain,
    spatial_kgain,
    temporal_shift,
    temporal_scale,
    temporal_qkv,
    temporal_qgain,
    temporal_kgain,
):
    vmem = pl.BlockSpec(memory_space=pltpu.VMEM)
    anywhere = pl.BlockSpec(memory_space=pl.ANY)
    dma = pltpu.SemaphoreType.DMA
    split = jnp.transpose(spatial_qkv, (0, 1, 3, 2, 4)).reshape(2, 3, 192, 1152)
    result = pl.pallas_call(
        fused_kernel,
        out_shape=jax.ShapeDtypeStruct((384, 1152), BF16),
        in_specs=[anywhere] * 4 + [vmem] * 7,
        out_specs=vmem,
        scratch_shapes=[
            pltpu.VMEM((9, 2, 3, 192, LANES), BF16),
            pltpu.VMEM((2, 192, 1152), BF16),
            pltpu.VMEM((1152, 1152), BF16),
            pltpu.VMEM((1152, 3456), BF16),
            pltpu.VMEM((4, 72, 384), F32),
            pltpu.VMEM((3, 1152, 384), F32),
            pltpu.VMEM((16, 3, 72, 384), BF16),
            pltpu.VMEM((2, 8, 3, 72, 384), BF16),
            pltpu.VMEM((2, 72, 1536), BF16),
            pltpu.VMEM((2, 1536, 72), BF16),
            pltpu.VMEM((2, 80, 1536), BF16),
            pltpu.VMEM((2, 1536, 768), F32),
            pltpu.VMEM((2, 8, 72, 384), BF16),
            pltpu.VMEM((16, 72, 384), BF16),
            pltpu.VMEM((96, SLAB, 1152), BF16),
            pltpu.VMEM((3, 32, SLAB, 1152), BF16),
            pltpu.VMEM((3, 1152, LANES), F32),
            pltpu.VMEM((1152, LANES), F32),
            pltpu.VMEM((3, 32, SLAB, 1152), BF16),
            pltpu.VMEM((96, SLAB, 1152), BF16),
            dma((3,)),
            dma((9,)),
            dma((3, 8)),
            dma((3, 8)),
            dma((2, 8)),
            dma((2, 8)),
            dma((3,)),
            dma((3,)),
            dma((3,)),
            dma((3,)),
        ],
        compiler_params=pltpu.CompilerParams(
            collective_id=0, has_side_effects=True, vmem_limit_bytes=62 * 1024 * 1024
        ),
        name="fused",
    )(
        split,
        residual.reshape(2, 192, 1152),
        spatial_proj,
        temporal_qkv,
        spatial_gate,
        temporal_shift,
        temporal_scale,
        spatial_qgain.reshape(1, 72),
        spatial_kgain.reshape(1, 72),
        temporal_qgain.reshape(1, 72),
        temporal_kgain.reshape(1, 72),
    )
    return result.reshape(2, 1, 192, 1152)


def solution(mesh):
    return jax.shard_map(
        per_device,
        mesh=mesh,
        in_specs=(
            P(None, "frame", "pos", None, None),
            P(None, "frame", "pos", None),
            P(),
            P(),
            P(),
            P(),
            P(),
            P(),
            P(),
            P(),
            P(),
        ),
        out_specs=P(None, "frame", "pos", None),
        check_vma=False,
    )
```

time: 123 us -> 107 us (0.87)
  Pallas kernels: 115 us -> 104 us
  local copies, waits for them, and re-layouts: 7.79 us -> 2.15 us
    pallas_call x2 -> x1, Pallas kernels: 115 us -> 104 us  [per_device(): pl.pallas_call(fused_kernel, out_shape=jax.ShapeDtypeStruct((384, 1152),...]
    reshape x5 -> x0, local copies, waits for them, and re-layouts: 7.79 us -> none  [the longest x1 2.36 us: per_device(): return result.reshape(2, 1, 192, 1152)]
    unnamed x0 -> x1, local copies, waits for them, and re-layouts: none -> 2.15 us
where the time goes in v2:
time: 107 us; the launch traced here: 106 us
  Pallas kernels  104 us (97%)
  local copies, waits for them, and re-layouts  2.15 us (2%)
    pallas_call x1, Pallas kernels, per_device(): pl.pallas_call(fused_kernel, out_shape=jax.ShapeDtypeStruct((384, 1152),...  104 us
    unnamed x1, local copies, waits for them, and re-layouts  2.15 us

profile of v2, /device:TPU:1, one launch (start us, length us, event | category | flops | bytes accessed | tf_op | source)
XLA Modules:
  0.0 106.5 jit_solution(17047749823422124104)
XLA Ops:
  0.0 104.3 %fused.1 = bf16[384,1152]{1,0:T(8,128)(2,1)} custom-call(bf16[2,3,192,1152]{3,2,1,0:T(8,128)(2,1)} %bitcast.14, bf16[2,192,1152]{2,1,0:T(8,128)(2,1)} %bitcast.15, bf16[1152,1152]{1,0:T(8,128)(2,1)} %proj_ref.1, bf16[1152,3456]{1,0:T(8,128)(2,1)} %weight_ref.1, f32[2,1152]{1,0:T(2,128)} %gate_ref.1, f32[2,1152]{1,0:T(2,128)} %shift_ref.1, ...), custom_call_target="tpu_custom_call" | custom-call | tf_op jit(solution)/shard_map/fused/pallas_call | solution.py:416
  104.3 2.1 %copy.15 = bf16[2,1,192,1152]{3,2,1,0:T(8,128)(2,1)} copy(bf16[2,1,192,1152]{3,2,1,0:T(8,128)(2,1)} %bitcast.13) | data formatting | bytes 1769472

commit v3 on v2

--- a/solution.py
+++ b/solution.py
@@ -66,6 +66,7 @@
     slab_recv_sem,
     slab_back_send_sem,
     slab_back_recv_sem,
+    known_sem,
 ):
     me = lax.axis_index("pos")
     frame = lax.axis_index("frame")
@@ -86,13 +87,27 @@
             barrier, inc=1, device_id={"pos": lax.rem(me + r, 8)}, device_id_type=MESH
         )
 
-    def greet(r, carry):
-        pl.semaphore_signal(
-            barrier, inc=1, device_id={"frame": lax.rem(frame + r, 32)}, device_id_type=MESH
-        )
-        return carry
-
-    lax.fori_loop(1, 32, greet, 0)
+    y, z, core = frame // 8, lax.rem(frame // 2, 4), lax.rem(frame, 2)
+
+    def at(y, z, core):
+        return (lax.rem(y, 4) * 4 + lax.rem(z, 4)) * 2 + lax.rem(core, 2)
+
+    beside_core = (at(y, z, core + 1),)
+    beside_y = (at(y + 1, z, core), at(y + 3, z, core))
+    beside_z = (at(y, z + 1, core), at(y, z + 3, core))
+    for neighbour in beside_core + beside_y + beside_z:
+        pl.semaphore_signal(barrier, inc=1, device_id={"frame": neighbour}, device_id_type=MESH)
+    rounds = (beside_core, beside_y, beside_z, beside_z)
+
+    def tell(n):
+        for neighbour in rounds[n]:
+            pl.semaphore_signal(
+                known_sem.at[n], inc=1, device_id={"frame": neighbour}, device_id_type=MESH
+            )
+
+    def hear(n):
+        pl.semaphore_wait(known_sem.at[n], len(rounds[n]))
+
     loads = [
         pltpu.make_async_copy(source, target, load_sem.at[n])
         for n, (source, target) in enumerate(
@@ -145,7 +160,8 @@
     turn(0)
     take(1).wait()
     turn(1)
-    pl.semaphore_wait(barrier, 38)
+    pl.semaphore_wait(barrier, 12)
+    tell(0)
 
     def feed(s, carry):
         @pl.when(s > 1)
@@ -164,6 +180,8 @@
         return carry
 
     lax.fori_loop(1, 9, feed, 0)
+    hear(0)
+    tell(1)
 
     def feed_second(r, carry):
         peer = lax.rem(me + r, 8)
@@ -172,6 +190,8 @@
         return carry
 
     lax.fori_loop(1, 8, feed_second, 0)
+    hear(1)
+    tell(2)
     for r in range(1, 8):
         exchange(2, lax.rem(me + r, 8), r).start()
     for h in range(2):
@@ -221,6 +241,9 @@
             await_pair(h, i)
             spread(h, i, 1)
             spread(h, i, 2)
+        hear(2 + h)
+        if h == 0:
+            tell(3)
         for g in range(2):
             for i in (2 * g, 2 * g + 1):
                 if h == 1:
@@ -449,6 +472,7 @@
             dma((3,)),
             dma((3,)),
             dma((3,)),
+            pltpu.SemaphoreType.REGULAR((4,)),
         ],
         compiler_params=pltpu.CompilerParams(
             collective_id=0, has_side_effects=True, vmem_limit_bytes=62 * 1024 * 1024

time: 107 us -> 104 us (0.972)
  Pallas kernels: 104 us -> 101 us
    pallas_call x1, Pallas kernels: 104 us -> 101 us  [per_device(): pl.pallas_call(fused_kernel, out_shape=jax.ShapeDtypeStruct((384, 1152),...]
where the time goes in v3:
time: 104 us
  Pallas kernels  101 us (97%)
  local copies, waits for them, and re-layouts  2.15 us (2%)
    pallas_call x1, Pallas kernels, per_device(): pl.pallas_call(fused_kernel, out_shape=jax.ShapeDtypeStruct((384, 1152),...  101 us
    unnamed x1, local copies, waits for them, and re-layouts  2.15 us

profile of v3, /device:TPU:1, one launch (start us, length us, event | category | flops | bytes accessed | tf_op | source)
XLA Modules:
  0.0 103.6 jit_solution(1291188597441705646)
XLA Ops:
  0.0 101.4 %fused.1 = bf16[384,1152]{1,0:T(8,128)(2,1)} custom-call(bf16[2,3,192,1152]{3,2,1,0:T(8,128)(2,1)} %bitcast.14, bf16[2,192,1152]{2,1,0:T(8,128)(2,1)} %bitcast.15, bf16[1152,1152]{1,0:T(8,128)(2,1)} %proj_ref.1, bf16[1152,3456]{1,0:T(8,128)(2,1)} %weight_ref.1, f32[2,1152]{1,0:T(2,128)} %gate_ref.1, f32[2,1152]{1,0:T(2,128)} %shift_ref.1, ...), custom_call_target="tpu_custom_call" | custom-call | tf_op jit(solution)/shard_map/fused/pallas_call | solution.py:439
  101.4 2.1 %copy.15 = bf16[2,1,192,1152]{3,2,1,0:T(8,128)(2,1)} copy(bf16[2,1,192,1152]{3,2,1,0:T(8,128)(2,1)} %bitcast.13) | data formatting | bytes 1769472

commit v4 on v3

--- a/solution.py
+++ b/solution.py
@@ -203,12 +203,13 @@
     lane = lax.broadcasted_iota(jnp.int32, (HEAD_DIM, LANES), 1)
     straight = (lane < 64) == ((jnp.zeros((HEAD_DIM, LANES), jnp.int32) + odd) == 0)
 
-    def give_back(h, r):
+    def give_back(h, r, tile):
+        span = pl.ds(128 * tile, 128)
         return pltpu.make_async_remote_copy(
-            src_ref=outgoing.at[h, r],
-            dst_ref=attended.at[2 * me + h],
-            send_sem=back_send_sem.at[h, r],
-            recv_sem=back_recv_sem.at[h, r],
+            src_ref=outgoing.at[h, r, :, span],
+            dst_ref=attended.at[2 * me + h, :, span],
+            send_sem=back_send_sem.at[h, r, tile],
+            recv_sem=back_recv_sem.at[h, r, tile],
             device_id={"pos": lax.rem(me + 8 - r, 8)},
             device_id_type=MESH,
         )
@@ -289,26 +290,23 @@
                             attended[2 * me + h, :, place] = piece.astype(BF16)
                         else:
                             outgoing[h, r, :, place] = piece.astype(BF16)
-                    if r > 0:
-                        give_back(h, r).start()
-
-    def arrived(h, r):
+            for tile in range(3):
+                for r in range(max(4 * g, 1), 4 * g + 4):
+                    give_back(h, r, tile).start()
+
+    def arrived(h, r, tile):
+        span = pl.ds(128 * tile, 128)
         return pltpu.make_async_remote_copy(
-            src_ref=outgoing.at[h, r],
-            dst_ref=attended.at[2 * lax.rem(me + r, 8) + h],
-            send_sem=back_send_sem.at[h, r],
-            recv_sem=back_recv_sem.at[h, r],
+            src_ref=outgoing.at[h, r, :, span],
+            dst_ref=attended.at[2 * lax.rem(me + r, 8) + h, :, span],
+            send_sem=back_send_sem.at[h, r, tile],
+            recv_sem=back_recv_sem.at[h, r, tile],
             device_id={"pos": lax.rem(me + r, 8)},
             device_id_type=MESH,
         )
 
     for load in loads:
         load.wait()
-    for h in range(2):
-        for r in range(1, 8):
-            arrived(h, r).wait_recv()
-    for n in range(16):
-        wide[0, 72 * n : 72 * n + 72, :] = attended[n].astype(F32)
     swap_rows = jnp.zeros((LANES, 1152), jnp.int32) + odd == 1
 
     def give_slab(i, r):
@@ -323,7 +321,13 @@
         )
 
     for tile in range(3):
-        rows = wide[0, :, 128 * tile : 128 * tile + 128].T
+        span = slice(128 * tile, 128 * tile + 128)
+        for h in range(2):
+            for r in range(1, 8):
+                arrived(h, r, tile).wait_recv()
+        for n in range(16):
+            wide[0, 72 * n : 72 * n + 72, span] = attended[n, :, span].astype(F32)
+        rows = wide[0, :, span].T
         if tile == 1:
             rows = jnp.where(swap_rows, jnp.concatenate([rows[64:], rows[:64]], axis=0), rows)
         mixed = jnp.dot(rows.astype(BF16), proj[...], preferred_element_type=F32)
@@ -404,7 +408,8 @@
             exchange(stage, lax.rem(me + r, 8), r).wait_send()
     for h in range(2):
         for r in range(1, 8):
-            give_back(h, r).wait_send()
+            for tile in range(3):
+                give_back(h, r, tile).wait_send()
     for i in range(3):
         all_of(
             slab_back.at[pl.ds(32 * i, 31)], slab_back_send_sem.at[i], slab_back_recv_sem.at[i]
@@ -466,8 +471,8 @@
             dma((9,)),
             dma((3, 8)),
             dma((3, 8)),
-            dma((2, 8)),
-            dma((2, 8)),
+            dma((2, 8, 3)),
+            dma((2, 8, 3)),
             dma((3,)),
             dma((3,)),
             dma((3,)),

time: 104 us -> 103 us (level)
  no operation moved by 1% of the time
where the time goes in v4:
time: 103 us
  Pallas kernels  101 us (98%)
  local copies, waits for them, and re-layouts  2.15 us (2%)
    pallas_call x1, Pallas kernels, per_device(): pl.pallas_call(fused_kernel, out_shape=jax.ShapeDtypeStruct((384, 1152),...  101 us
    unnamed x1, local copies, waits for them, and re-layouts  2.15 us

profile of v4, /device:TPU:1, one launch (start us, length us, event | category | flops | bytes accessed | tf_op | source)
XLA Modules:
  0.0 102.7 jit_solution(15067071327796113095)
XLA Ops:
  0.0 100.5 %fused.1 = bf16[384,1152]{1,0:T(8,128)(2,1)} custom-call(bf16[2,3,192,1152]{3,2,1,0:T(8,128)(2,1)} %bitcast.14, bf16[2,192,1152]{2,1,0:T(8,128)(2,1)} %bitcast.15, bf16[1152,1152]{1,0:T(8,128)(2,1)} %proj_ref.1, bf16[1152,3456]{1,0:T(8,128)(2,1)} %weight_ref.1, f32[2,1152]{1,0:T(2,128)} %gate_ref.1, f32[2,1152]{1,0:T(2,128)} %shift_ref.1, ...), custom_call_target="tpu_custom_call" | custom-call | tf_op jit(solution)/shard_map/fused/pallas_call | solution.py:444
  100.5 2.1 %copy.15 = bf16[2,1,192,1152]{3,2,1,0:T(8,128)(2,1)} copy(bf16[2,1,192,1152]{3,2,1,0:T(8,128)(2,1)} %bitcast.13) | data formatting | bytes 1769472

commit v5 on v4

--- a/solution.py
+++ b/solution.py
@@ -67,6 +67,8 @@
     slab_back_send_sem,
     slab_back_recv_sem,
     known_sem,
+    staged,
+    store_sem,
 ):
     me = lax.axis_index("pos")
     frame = lax.axis_index("frame")
@@ -403,6 +405,12 @@
 
         lax.fori_loop(1, 32, return_slab, 0)
         slab_back[32 * i + frame] = slab_outgoing[i, 0]
+
+    def store(i):
+        return pltpu.make_async_copy(
+            staged.at[i], out_ref.at[pl.ds(128 * i, 128)], store_sem.at[i]
+        )
+
     for stage in range(3):
         for r in range(1, 8):
             exchange(stage, lax.rem(me + r, 8), r).wait_send()
@@ -414,8 +422,10 @@
         all_of(
             slab_back.at[pl.ds(32 * i, 31)], slab_back_send_sem.at[i], slab_back_recv_sem.at[i]
         ).wait_recv()
-        out_ref[128 * i : 128 * i + 128, :] = slab_back[32 * i : 32 * i + 32].reshape(128, 1152)
+        staged[i] = slab_back[32 * i : 32 * i + 32].reshape(128, 1152)
+        store(i).start()
     for i in range(3):
+        store(i).wait()
         all_of(
             slab_recv.at[i, pl.ds(1, 31)], slab_send_sem.at[i], slab_recv_sem.at[i]
         ).wait_send()
@@ -445,7 +455,7 @@
         fused_kernel,
         out_shape=jax.ShapeDtypeStruct((384, 1152), BF16),
         in_specs=[anywhere] * 4 + [vmem] * 7,
-        out_specs=vmem,
+        out_specs=anywhere,
         scratch_shapes=[
             pltpu.VMEM((9, 2, 3, 192, LANES), BF16),
             pltpu.VMEM((2, 192, 1152), BF16),
@@ -478,6 +488,8 @@
             dma((3,)),
             dma((3,)),
             pltpu.SemaphoreType.REGULAR((4,)),
+            pltpu.VMEM((3, 128, 1152), BF16),
+            dma((3,)),
         ],
         compiler_params=pltpu.CompilerParams(
             collective_id=0, has_side_effects=True, vmem_limit_bytes=62 * 1024 * 1024

time: 103 us -> 102 us (level)
  no operation moved by 1% of the time
where the time goes in v5:
time: 102 us
  Pallas kernels  100 us (98%)
  local copies, waits for them, and re-layouts  2.15 us (2%)
    pallas_call x1, Pallas kernels, per_device(): pl.pallas_call(fused_kernel, out_shape=jax.ShapeDtypeStruct((384, 1152),...  100 us
    unnamed x1, local copies, waits for them, and re-layouts  2.15 us

profile of v5, /device:TPU:1, one launch (start us, length us, event | category | flops | bytes accessed | tf_op | source)
XLA Modules:
  0.0 102.3 jit_solution(906089340330005256)
XLA Ops:
  0.0 100.2 %fused.1 = bf16[384,1152]{1,0:T(8,128)(2,1)} custom-call(bf16[2,3,192,1152]{3,2,1,0:T(8,128)(2,1)} %bitcast.14, bf16[2,192,1152]{2,1,0:T(8,128)(2,1)} %bitcast.15, bf16[1152,1152]{1,0:T(8,128)(2,1)} %proj_ref.1, bf16[1152,3456]{1,0:T(8,128)(2,1)} %weight_ref.1, f32[2,1152]{1,0:T(2,128)} %gate_ref.1, f32[2,1152]{1,0:T(2,128)} %shift_ref.1, ...), custom_call_target="tpu_custom_call" | custom-call | tf_op jit(solution)/shard_map/fused/pallas_call | solution.py:454
  100.2 2.1 %copy.15 = bf16[2,1,192,1152]{3,2,1,0:T(8,128)(2,1)} copy(bf16[2,1,192,1152]{3,2,1,0:T(8,128)(2,1)} %bitcast.13) | data formatting | bytes 1769472
